TPU v7x, 32 devices: a whole 2x2x4 slice. The times are simulated.
32 devices in a mesh: lat: 4 (over x, core), lon: 8 (over z, y).
Axes of the slice: x: 2, y: 2, z: 4, core: 2. Of those that a mesh axis runs over, the one named last changes fastest.
Arguments:
- prediction_fields: float32 [4, 69, 360, 512], P(None, None, 'lon', 'lat'), may hold values from -16 to 16
- verifying_state: float32 [69, 360, 512], P(None, 'lon', 'lat'), may hold values from -16 to 16
- normal_state: float32 [69, 360, 512], P(None, 'lon', 'lat'), may hold values from -16 to 16
- evaluated_point_flag: int32 [360, 512], P('lon', 'lat'), may hold values 0 or 1
- parallels_each_strip: int32 [4], replicated, may hold values from 1 to 128, 361 in all
Outputs:
- parallel_quadratic_error: float32 [4, 69, 512], P(None, None, 'lat')
- parallel_systematic_error: float32 [4, 69, 512], P(None, None, 'lat')
- parallel_pattern_skill: float32 [4, 69, 512], P(None, None, 'lat')
- rmse: float32 [4, 69], replicated
- systematic_error: float32 [4, 69], replicated
- pattern_skill: float32 [4, 69], replicated
Inputs may be any that keep to these rules, and one draw needn't show every extreme that they name: `parallels_each_strip`: they sum to 361, and some band holds exactly 128 rows.
All inputs are finite; a program needn't handle non-finite values.
Results may differ from a plain program's by a relative error of at most 0.00002.
Values sent between devices are 32-bit elements.
A program may use at most 64 MiB of HBM per device.

v0:
```python
import functools
import math

import jax
import jax.numpy as jnp
from jax import lax
from jax.experimental import pallas as pl
from jax.experimental.pallas import tpu as pltpu
from jax.sharding import PartitionSpec as P

MEAN_ROWS = 90
FLOOR = 0.1
MESH = pl.DeviceIdType.MESH


def cosine(y):
    y2 = y * y
    terms = [(-1) ** k / math.factorial(2 * k) for k in range(9)]
    total = jnp.full_like(y, terms[-1])
    for term in terms[-2::-1]:
        total = total * y2 + term
    return total


def kernel(n_lat, n_lon, vp, par, pred, ver, norm, flag, o_sq, o_off, o_skill, g_rmse, g_off, g_skill,
           xp, xv, xn, xf, kf, spread_t, part, one_in, two_out, two_in, tot, flat, fin, g_out, g_in, g_mine, g_all, g_tmp,
           in_sem, pred_sem, one_s, one_r, two_s, two_r, agz_s, agz_r, agy_s, agy_r, lat_s, lat_r, lon_s, lon_r):
    nvars, cols, leads, lanes = pred.shape
    pair = 2 if n_lon % 2 == 0 else 1
    outer = n_lon // pair
    band = lax.axis_index("lat")
    me = lax.axis_index("lon")
    a, b = me // pair, me % pair
    ob = (pair - 1) - b
    lv = leads * vp
    blocks = part.shape[1]

    starts = [min(d * vp, nvars - vp) for d in range(n_lon)]

    def first_var(d):
        return jnp.minimum(d * vp, nvars - vp)

    def other(k):
        return lax.rem(a + k, outer)

    steps = [k for k in range(1, outer)] + [0]
    order = [(k, True) for k in steps] if pair == 2 else []
    order += [(k, False) for k in steps]
    first = [
        pltpu.make_async_copy(flag, xf, in_sem.at[0]),
        pltpu.make_async_copy(norm, xn, in_sem.at[1]),
        pltpu.make_async_copy(ver, xv, in_sem.at[2]),
    ]
    for c in first:
        c.start()
    chunk_vars, copies = [], []
    for i, (k, away) in enumerate(order):
        v0 = first_var(other(k) * pair + (ob if away else b))
        c = pltpu.make_async_copy(pred.at[pl.ds(v0, vp)], xp.at[i], pred_sem.at[i])
        c.start()
        chunk_vars.append(v0)
        copies.append(c)

    barrier = pltpu.get_barrier_semaphore()
    for k in range(1, n_lon):
        pl.semaphore_signal(barrier, inc=1, device_id=(band, lax.rem(me + k, n_lon)), device_id_type=MESH)
    for k in range(1, n_lat):
        pl.semaphore_signal(barrier, inc=1, device_id=(lax.rem(band + k, n_lat), me), device_id_type=MESH)

    first_row = jnp.int32(0)
    filled = jnp.int32(0)
    for i in range(n_lat):
        first_row = first_row + jnp.where(i < band, par[i], 0)
        filled = filled + jnp.where(i == band, par[i], 0)
    total_rows = MEAN_ROWS * n_lat + 1
    slot = lax.broadcasted_iota(jnp.int32, (8, lanes), 1)
    g = (first_row + slot).astype(jnp.float32)
    normalizer = sum(math.sin(math.pi * r / (total_rows - 1)) for r in range(total_rows))
    angle = (g - 0.5 * (total_rows - 1)) * (math.pi / (total_rows - 1))
    weight = jnp.where(slot < filled, cosine(angle) * (total_rows / normalizer), 0.0)
    if vp % 4:
        for i in range(n_lon):
            part[i, blocks - 1] = jnp.zeros((4, lanes), jnp.float32)

    first[0].wait()
    kf[...] = jnp.where(lax.broadcasted_iota(jnp.int32, (cols, lanes), 1) < filled, xf[...].astype(jnp.float32), 0.0)
    first[1].wait()
    first[2].wait()

    def truth_column(c, total):
        t = kf[pl.ds(c, 1), :] * (xv[c] - xn[c])
        xv[c] = t
        return total + t * t

    spread_t[...] = lax.fori_loop(0, cols, truth_column, jnp.zeros((nvars, lanes), jnp.float32))

    def sums(i):
        copies[i].wait()
        v0 = chunk_vars[i]

        def one(v, carry):
            sq = off = pr = sp = None
            for c in range(cols):
                n_ = xn[c, pl.ds(v0 + v, 1), :]
                t_ = xv[c, pl.ds(v0 + v, 1), :]
                f = kf[c:c + 1, :] * (xp[i, v, c] - n_)
                e = f - t_
                if sq is None:
                    sq, off, pr, sp = e * e, e, f * t_, f * f
                else:
                    sq, off, pr, sp = sq + e * e, off + e, pr + f * t_, sp + f * f
            part[i, v] = sq
            part[i, vp + v] = off
            part[i, 2 * vp + v] = pr
            part[i, 3 * vp + v] = sp
            return carry

        lax.fori_loop(0, vp, one, 0)
        for v in range(vp):
            part[i, 4 * vp + v // 4, v % 4:v % 4 + 1, :] = spread_t[pl.ds(v0 + v, 1), :]

    def remote(src, dst, s, r, device):
        return pltpu.make_async_remote_copy(src_ref=src, dst_ref=dst, send_sem=s, recv_sem=r, device_id=device, device_id_type=MESH)

    partner = (band, a * pair + ob)
    sent = []
    phase_one = {}
    greeted = False
    for i, (k, away) in enumerate(order):
        sums(i)
        if not greeted:
            pl.semaphore_wait(barrier, n_lon - 1 + n_lat - 1)
            greeted = True
        if away:
            c = remote(part.at[i], one_in.at[k], one_s.at[k], one_r.at[k], partner)
            c.start()
            phase_one[k] = c
            sent.append(c)
    phase_two = {}
    base = len(order) - outer
    for q, k in enumerate(steps):
        local = part[base + q]
        if pair == 2:
            phase_one[k].wait_recv()
            local = local + one_in[k]
        if k:
            two_out[k] = local
            c = remote(two_out.at[k], two_in.at[k], two_s.at[k], two_r.at[k], (band, other(k) * pair + b))
            c.start()
            phase_two[k] = c
            sent.append(c)
        else:
            tot[...] = local
    for k in range(1, outer):
        phase_two[k].wait_recv()
    total = tot[...]
    for k in range(1, outer):
        total = total + two_in[k]
    tot[...] = total

    points = 1.0 / float(cols * n_lon)
    for v in range(vp):
        sq, off, pr, sp = [tot[s * vp + v] for s in range(4)]
        tr = jnp.broadcast_to(tot[4 * vp + v // 4, v % 4:v % 4 + 1, :], (leads, lanes))
        for s, x in enumerate((sq, off, pr, sp, tr)):
            flat[s, pl.ds(v, leads, stride=vp), :] = x
    g_out[...] = jnp.zeros_like(g_out)
    for s in range(5):
        d = lax.dot_general(weight, flat[s], (((1,), (1,)), ((), ())), precision=lax.Precision.HIGHEST,
                            preferred_element_type=jnp.float32)
        g_out[s:s + 1, 0:lv] = d[0:1, :]
    lat_copies = []
    for k in range(1, n_lat):
        c = remote(g_out, g_in.at[k], lat_s.at[k], lat_r.at[k], (lax.rem(band + k, n_lat), me))
        c.start()
        lat_copies.append(c)
        sent.append(c)

    for v in range(vp):
        sq, off, pr, sp = [tot[s * vp + v] * points for s in range(4)]
        tr = jnp.broadcast_to(tot[4 * vp + v // 4, v % 4:v % 4 + 1, :], (leads, lanes)) * points
        fin[me, v] = sq
        fin[me, vp + v] = off
        fin[me, 2 * vp + v] = pr / jnp.sqrt(jnp.maximum(sp, FLOOR) * jnp.maximum(tr, FLOOR))
    gather_z, gather_y = {}, {}
    if pair == 2:
        c = remote(fin.at[me], fin.at[me], agy_s.at[0], agy_r.at[0], partner)
        c.start()
        gather_y[0] = c
        sent.append(c)
    for k in range(1, outer):
        c = remote(fin.at[me], fin.at[me], agz_s.at[k], agz_r.at[k], (band, other(k) * pair + b))
        c.start()
        gather_z[k] = c
        sent.append(c)

    for c in lat_copies:
        c.wait_recv()
    gs = g_out[...]
    for k in range(1, n_lat):
        gs = gs + g_in[k]
    gs = gs / float(total_rows * cols * n_lon)
    g_mine[...] = gs
    g_all[me, 0:1, :] = jnp.sqrt(jnp.maximum(g_mine[0:1, :], FLOOR))
    g_all[me, 1:2, :] = g_mine[1:2, :]
    g_all[me, 2:3, :] = g_mine[2:3, :] / jnp.sqrt(
        jnp.maximum(g_mine[3:4, :], FLOOR) * jnp.maximum(g_mine[4:5, :], FLOOR))
    g_all[me, 3:8, :] = jnp.zeros((5, g_all.shape[2]), jnp.float32)
    lon_copies = []
    for k in range(1, n_lon):
        c = remote(g_all.at[me], g_all.at[me], lon_s.at[k], lon_r.at[k], (band, lax.rem(me + k, n_lon)))
        c.start()
        lon_copies.append(c)
        sent.append(c)

    for k in sorted(range(1, outer), key=lambda k: min(k, outer - k)):
        gather_z[k].wait_recv()
        if pair == 2:
            source = fin.at[lax.rem(a - k + outer, outer) * pair + b]
            c = remote(source, source, agy_s.at[k], agy_r.at[k], partner)
            c.start()
            gather_y[k] = c
            sent.append(c)
    for c in lon_copies:
        c.wait_recv()
    for d in range(n_lon):
        for l in range(leads):
            g_tmp[l, 0:3, starts[d]:starts[d] + vp] = g_all[d, 0:3, l * vp:(l + 1) * vp]
    for l in range(leads):
        for m, out in enumerate((g_rmse, g_off, g_skill)):
            out[l:l + 1, :] = g_tmp[l, m:m + 1, 0:nvars]
    for k in gather_y:
        gather_y[k].wait_recv()
    for d in range(n_lon):
        for m, out in enumerate((o_sq, o_off, o_skill)):
            out[starts[d]:starts[d] + vp] = fin[d, m * vp:(m + 1) * vp]
    for c in sent:
        c.wait_send()


def local(n_lat, n_lon, pred, ver, norm, flag, par):
    leads, nvars, cols, lanes = pred.shape
    vp = -(-nvars // n_lon)
    outer = n_lon // 2 if n_lon % 2 == 0 else n_lon
    blocks = 4 * vp + -(-vp // 4)
    glanes = -(-leads * vp // 128) * 128
    f32 = jnp.float32
    dma = pltpu.SemaphoreType.DMA
    vmem = pl.BlockSpec(memory_space=pltpu.VMEM)
    hbm = pl.BlockSpec(memory_space=pl.ANY)
    zonal = jax.ShapeDtypeStruct((nvars, leads, lanes), f32)
    whole = jax.ShapeDtypeStruct((leads, nvars), f32)
    out = pl.pallas_call(
        functools.partial(kernel, n_lat, n_lon, vp),
        out_shape=(zonal,) * 3 + (whole,) * 3,
        in_specs=[pl.BlockSpec(memory_space=pltpu.SMEM)] + [hbm] * 4,
        out_specs=(vmem,) * 6,
        scratch_shapes=[
            pltpu.VMEM((n_lon, vp, cols, leads, lanes), f32),
            pltpu.VMEM((cols, nvars, lanes), f32),
            pltpu.VMEM((cols, nvars, lanes), f32),
            pltpu.VMEM((cols, lanes), jnp.int32),
            pltpu.VMEM((cols, lanes), f32),
            pltpu.VMEM((nvars, lanes), f32),
            pltpu.VMEM((n_lon, blocks, 4, lanes), f32),
            pltpu.VMEM((outer, blocks, 4, lanes), f32),
            pltpu.VMEM((outer, blocks, 4, lanes), f32),
            pltpu.VMEM((outer, blocks, 4, lanes), f32),
            pltpu.VMEM((blocks, 4, lanes), f32),
            pltpu.VMEM((5, leads * vp, lanes), f32),
            pltpu.VMEM((n_lon, 3 * vp, leads, lanes), f32),
            pltpu.VMEM((8, glanes), f32),
            pltpu.VMEM((n_lat, 8, glanes), f32),
            pltpu.VMEM((8, glanes), f32),
            pltpu.VMEM((n_lon, 8, glanes), f32),
            pltpu.VMEM((leads, 8, 128 * (-(-nvars // 128))), f32),
            dma((3,)), dma((n_lon,)),
            dma((outer,)), dma((outer,)), dma((outer,)), dma((outer,)),
            dma((outer,)), dma((outer,)), dma((outer,)), dma((outer,)),
            dma((n_lat,)), dma((n_lat,)), dma((n_lon,)), dma((n_lon,)),
        ],
        compiler_params=pltpu.CompilerParams(collective_id=0, has_side_effects=True),
    )(par, jnp.transpose(pred, (1, 2, 0, 3)), jnp.transpose(ver, (1, 0, 2)), jnp.transpose(norm, (1, 0, 2)), flag)
    return tuple(jnp.transpose(x, (1, 0, 2)) for x in out[:3]) + tuple(out[3:])


def solution(mesh):
    n_lat, n_lon = mesh.shape["lat"], mesh.shape["lon"]
    in_specs = (
        P(None, None, "lon", "lat"),
        P(None, "lon", "lat"),
        P(None, "lon", "lat"),
        P("lon", "lat"),
        P(),
    )
    out_specs = (P(None, None, "lat"), P(None, None, "lat"), P(None, None, "lat"), P(), P(), P())
    return jax.shard_map(functools.partial(local, n_lat, n_lon), mesh=mesh, in_specs=in_specs, out_specs=out_specs,
                         check_vma=False)
```

profile of v0, /device:TPU:0, one launch (start us, length us, event | category | flops | bytes accessed | tf_op | source)
XLA Modules:
  0.0 41.8 jit_solution(4445704036245968110)
XLA Ops:
  0.6 32.7 %shard_map.100 = (f32[69,4,128]{2,1,0:T(4,128)}, f32[69,4,128]{2,1,0:T(4,128)}, f32[69,4,128]{2,1,0:T(4,128)}, f32[4,69]{1,0:T(4,128)}, f32[4,69]{1,0:T(4,128)}, /*index=5*/f32[4,69]{1,0:T(4,128)}) custom-call(s32[4]{0:T(128)} %par.1, f32[69,45,4,128]{3,2,1,0:T(4,128)} %bitcast.6, f32[45,69,128]{2,1,0:T(8,128)} %bitcast.7, f32[45,69,128]{2,1,0:T(8,128)} %bitcast.8, ...), custom_call_target="tpu_custom_call" | custom-call | tf_op jit(solution)/shard_map/pallas_call | solution.py:253
  33.4 1.6 %copy.17 = f32[4,69,128]{2,0,1:T(4,128)} copy(f32[4,69,128]{2,0,1:T(4,128)} %bitcast.11) | data formatting | bytes 282624
  34.9 1.6 %copy.18 = f32[4,69,128]{2,0,1:T(4,128)} copy(f32[4,69,128]{2,0,1:T(4,128)} %bitcast.10) | data formatting | bytes 282624
  36.5 1.6 %copy.19 = f32[4,69,128]{2,0,1:T(4,128)} copy(f32[4,69,128]{2,0,1:T(4,128)} %bitcast.9) | data formatting | bytes 282624
  38.1 1.3 %copy.20 = f32[4,69]{1,0:T(4,128)} copy(f32[4,69]{1,0:T(4,128)} %get-tuple-element.27) | data formatting | bytes 2208
  39.3 1.3 %copy.21 = f32[4,69]{1,0:T(4,128)} copy(f32[4,69]{1,0:T(4,128)} %get-tuple-element.28) | data formatting | bytes 2208
  40.6 1.2 %copy.22 = f32[4,69]{1,0:T(4,128)} copy(f32[4,69]{1,0:T(4,128)} %get-tuple-element.29) | data formatting | bytes 2208
where the time goes:
time: 42.1 us; the launch traced here: 41.8 us
  Pallas kernels  32.7 us (78%)
  local copies, waits for them, and re-layouts  8.48 us (20%)
  between operations  0.64 us (2%)
    pallas_call x1, Pallas kernels, local(): pl.pallas_call(functools.partial(kernel, n_lat, n_lon, vp), out_shape=(zo...  32.7 us
    unnamed x6, local copies, waits for them, and re-layouts  8.48 us

commit v1 on v0

--- a/solution.py
+++ b/solution.py
@@ -10,6 +10,7 @@
 
 MEAN_ROWS = 90
 FLOOR = 0.1
+LIMIT = 58 << 20
 MESH = pl.DeviceIdType.MESH
 
 
@@ -238,6 +239,15 @@
         c.wait_send()
 
 
+def writer(a, b, c, d, e, f, *rest):
+    sem = rest[6]
+    copies = [pltpu.make_async_copy(x, y, sem.at[i]) for i, (x, y) in enumerate(zip((a, b, c, d, e, f), rest[:6]))]
+    for c in copies:
+        c.start()
+    for c in copies:
+        c.wait()
+
+
 def local(n_lat, n_lon, pred, ver, norm, flag, par):
     leads, nvars, cols, lanes = pred.shape
     vp = -(-nvars // n_lon)
@@ -252,7 +262,7 @@
     whole = jax.ShapeDtypeStruct((leads, nvars), f32)
     out = pl.pallas_call(
         functools.partial(kernel, n_lat, n_lon, vp),
-        out_shape=(zonal,) * 3 + (whole,) * 3,
+        out_shape=(pltpu.VMEM((nvars, leads, lanes), f32),) * 3 + (pltpu.VMEM((leads, nvars), f32),) * 3,
         in_specs=[pl.BlockSpec(memory_space=pltpu.SMEM)] + [hbm] * 4,
         out_specs=(vmem,) * 6,
         scratch_shapes=[
@@ -279,8 +289,16 @@
             dma((outer,)), dma((outer,)), dma((outer,)), dma((outer,)),
             dma((n_lat,)), dma((n_lat,)), dma((n_lon,)), dma((n_lon,)),
         ],
-        compiler_params=pltpu.CompilerParams(collective_id=0, has_side_effects=True),
+        compiler_params=pltpu.CompilerParams(collective_id=0, has_side_effects=True, vmem_limit_bytes=LIMIT),
     )(par, jnp.transpose(pred, (1, 2, 0, 3)), jnp.transpose(ver, (1, 0, 2)), jnp.transpose(norm, (1, 0, 2)), flag)
+    out = pl.pallas_call(
+        writer,
+        out_shape=(zonal,) * 3 + (whole,) * 3,
+        in_specs=[vmem] * 6,
+        out_specs=(hbm,) * 6,
+        scratch_shapes=[dma((6,))],
+        compiler_params=pltpu.CompilerParams(vmem_limit_bytes=4 << 20),
+    )(*out)
     return tuple(jnp.transpose(x, (1, 0, 2)) for x in out[:3]) + tuple(out[3:])
 
 

time: 42.1 us -> 33.6 us (0.80)
  local copies, waits for them, and re-layouts: 8.48 us -> 0 us
    unnamed x6 -> x0, local copies, waits for them, and re-layouts: 8.48 us -> none
    pallas_call x1 -> x2, Pallas kernels: 32.7 us -> 32.8 us  [the longest x1 31.9 us: local(): pl.pallas_call(functools.partial(kernel, n_lat, n_lon, vp), out_shape=(pl...]
where the time goes in v1:
time: 33.6 us; the launch traced here: 33.4 us
  Pallas kernels  32.8 us (98%)
  between operations  0.64 us (2%)
    pallas_call x1, Pallas kernels, local(): pl.pallas_call(functools.partial(kernel, n_lat, n_lon, vp), out_shape=(pl...  31.9 us
    pallas_call x1, Pallas kernels, local(): pl.pallas_call(writer, out_shape=(zonal,) * 3 + (whole,) * 3, in_specs=[v...  0.81 us

profile of v1, /device:TPU:0, one launch (start us, length us, event | category | flops | bytes accessed | tf_op | source)
XLA Modules:
  0.0 33.4 jit_solution(7309494892705363506)
XLA Ops:
  0.6 31.9 %shard_map.100 = (f32[69,4,128]{2,1,0:T(4,128)S(1)}, f32[69,4,128]{2,1,0:T(4,128)S(1)}, f32[69,4,128]{2,1,0:T(4,128)S(1)}, f32[4,69]{1,0:T(4,128)S(1)}, f32[4,69]{1,0:T(4,128)S(1)}, /*index=5*/f32[4,69]{1,0:T(4,128)S(1)}) custom-call(s32[4]{0:T(128)} %par.1, f32[69,45,4,128]{3,2,1,0:T(4,128)} %bitcast.6, f32[45,69,128]{2,1,0:T(8,128)} %bitcast.7, ...), custom_call_target="tpu_custom_call" | custom-call | tf_op jit(solution)/shard_map/pallas_call | solution.py:263
  32.6 0.8 %shard_map.101 = (f32[69,4,128]{2,1,0:T(4,128)}, f32[69,4,128]{2,1,0:T(4,128)}, f32[69,4,128]{2,1,0:T(4,128)}, f32[4,69]{1,0:T(4,128)}, f32[4,69]{1,0:T(4,128)}, /*index=5*/f32[4,69]{1,0:T(4,128)}) custom-call(f32[69,4,128]{2,1,0:T(4,128)S(1)} %get-tuple-element.18.a, f32[69,4,128]{2,1,0:T(4,128)S(1)} %get-tuple-element.19.b, ...), custom_call_target="tpu_custom_call" | custom-call | tf_op jit(solution)/shard_map/pallas_call | solution.py:294

commit v2 on v1

v2 whole, which is shorter than its diff:
```python
import functools
import math

import jax
import jax.numpy as jnp
from jax import lax
from jax.experimental import pallas as pl
from jax.experimental.pallas import tpu as pltpu
from jax.sharding import PartitionSpec as P

MEAN_ROWS = 90
FLOOR = 0.1
MESH = pl.DeviceIdType.MESH
LIMIT = 58 << 20


def cosine(y):
    y2 = y * y
    terms = [(-1) ** k / math.factorial(2 * k) for k in range(9)]
    total = jnp.full_like(y, terms[-1])
    for term in terms[-2::-1]:
        total = total * y2 + term
    return total


def split(n_lon, vp):
    pair = 2 if n_lon % 2 == 0 else 1
    groups = max(g for g in (1, 2, 3) if vp % g == 0)
    return pair, n_lon // pair, groups


def kernel(n_lat, n_lon, vp, par, pred, ver, norm, flag, zon, g_rmse, g_off, g_skill,
           xp, xv, xn, xf, kf, spread_t, part, one_in, two_out, two_in, flat, g_out, g_in, g_mine,
           in_sem, pred_sem, out_s, one_r, two_r, agz_r, agy_r, g_r):
    nvars, cols, leads, lanes = pred.shape
    pair, outer, groups = split(n_lon, vp)
    gv = vp // groups
    gb = 4 * gv - (-gv // leads)
    band = lax.axis_index("lat")
    me = lax.axis_index("lon")
    a, b = me // pair, me % pair
    ob = (pair - 1) - b
    wide = flat.shape[1] // leads
    paired = outer & (outer - 1) == 0

    def first_var(d):
        return jnp.minimum(d * vp, nvars - vp)

    def flip(k):
        other, bit = a, 1
        while bit <= k:
            if k & bit:
                other = other + bit * (1 - 2 * ((a // bit) % 2))
            bit *= 2
        return other

    def to(k):
        return flip(k) if paired else lax.rem(a + k, outer)

    def source(k):
        return flip(k) if paired else lax.rem(a - k + outer, outer)

    far = list(range(outer - 1, 0, -1))
    steps = far + [0]
    order = [(k, True) for k in steps] if pair == 2 else []
    base = len(order)
    order += [(k, False) for k in steps]
    barrier = pltpu.get_barrier_semaphore()
    for k in range(1, n_lon):
        pl.semaphore_signal(barrier, inc=1, device_id=(band, lax.rem(me + k, n_lon)), device_id_type=MESH)
    for k in range(1, n_lat):
        pl.semaphore_signal(barrier, inc=1, device_id=(lax.rem(band + k, n_lat), me), device_id_type=MESH)

    first = [
        pltpu.make_async_copy(flag, xf, in_sem.at[0]),
        pltpu.make_async_copy(norm, xn, in_sem.at[1]),
        pltpu.make_async_copy(ver, xv, in_sem.at[2]),
    ]
    for c in first:
        c.start()
    chunk_vars, copies = [], []
    for i, (k, away) in enumerate(order):
        v0 = first_var(to(k) * pair + (ob if away else b))
        chunk_vars.append(v0)
        copies.append(pltpu.make_async_copy(pred.at[pl.ds(v0, vp)], xp.at[i], pred_sem.at[i]))
    copies[0].start()

    first_row = jnp.int32(0)
    filled = jnp.int32(0)
    for i in range(n_lat):
        first_row = first_row + jnp.where(i < band, par[i], 0)
        filled = filled + jnp.where(i == band, par[i], 0)
    total_rows = MEAN_ROWS * n_lat + 1
    slot = lax.broadcasted_iota(jnp.int32, (8, lanes), 1)
    g_row = (first_row + slot).astype(jnp.float32)
    normalizer = sum(math.sin(math.pi * r / (total_rows - 1)) for r in range(total_rows))
    angle = (g_row - 0.5 * (total_rows - 1)) * (math.pi / (total_rows - 1))
    weight = jnp.where(slot < filled, cosine(angle) * (total_rows / normalizer), 0.0)
    if gv % leads:
        for i in range(n_lon):
            for g in range(groups):
                part[i, g * gb + gb - 1] = jnp.zeros((leads, lanes), jnp.float32)

    first[0].wait()
    kf[...] = jnp.where(lax.broadcasted_iota(jnp.int32, (cols, lanes), 1) < filled, xf[...].astype(jnp.float32), 0.0)
    first[1].wait()
    first[2].wait()
    for c in copies[1:]:
        c.start()

    def truth_column(c, total):
        t = kf[pl.ds(c, 1), :] * (xv[c] - xn[c])
        xv[c] = t
        return total + t * t

    spread_t[...] = lax.fori_loop(0, cols, truth_column, jnp.zeros((nvars, lanes), jnp.float32))

    def sums(i):
        copies[i].wait()
        v0 = chunk_vars[i]

        def one(v, carry):
            sq = off = pr = sp = None
            for c in range(cols):
                n_ = xn[c, pl.ds(v0 + v, 1), :]
                t_ = xv[c, pl.ds(v0 + v, 1), :]
                f = kf[c:c + 1, :] * (xp[i, v, c] - n_)
                e = f - t_
                if sq is None:
                    sq, off, pr, sp = e * e, e, f * t_, f * f
                else:
                    sq, off, pr, sp = sq + e * e, off + e, pr + f * t_, sp + f * f
            row = v * 4 + (v // gv) * (gb - 4 * gv)
            part[i, row] = sq
            part[i, row + 1] = off
            part[i, row + 2] = pr
            part[i, row + 3] = sp
            tr = jnp.broadcast_to(spread_t[pl.ds(v0 + v, 1), :], (leads, lanes))
            for s, x in enumerate((sq, off, pr, sp, tr)):
                flat[s, pl.ds(v0 + v, leads, stride=wide), :] = x
            return carry

        lax.fori_loop(0, vp, one, 0)
        for v in range(vp):
            g, r = divmod(v, gv)
            part[i, g * gb + 4 * gv + r // leads, r % leads:r % leads + 1, :] = spread_t[pl.ds(v0 + v, 1), :]

    def block(g):
        return pl.ds(g * gb, gb)

    def send(src, dst, s, r, device):
        c = pltpu.make_async_remote_copy(src_ref=src, dst_ref=dst, send_sem=s, recv_sem=r, device_id=device, device_id_type=MESH)
        c.start()
        return c

    def await_bytes(ref, s):
        pltpu.make_async_copy(ref, ref, s).wait()

    partner = (band, a * pair + ob)
    phase_one, gather_z = {}, {}

    def send_one(g, q, k):
        phase_one[g, k] = send(part.at[q, block(g)], one_in.at[k, block(g)], out_s.at[0], one_r.at[g, k], partner)

    greeted = False
    for q, k in enumerate(steps if pair == 2 else []):
        sums(q)
        if not greeted:
            pl.semaphore_wait(barrier, n_lon - 1 + n_lat - 1)
            greeted = True
        send_one(0, q, k)
    for g in range(1, groups):
        for q, k in enumerate(steps if pair == 2 else []):
            send_one(g, q, k)

    def stage_a(g):
        for q, k in enumerate(steps):
            if g == 0:
                sums(base + q)
                if base == 0 and q == 0:
                    pl.semaphore_wait(barrier, n_lon - 1 + n_lat - 1)
            local = part[base + q, block(g)]
            if pair == 2:
                phase_one[g, k].wait_recv()
                local = local + one_in[k, block(g)]
            two_out[k, block(g)] = local
            if k:
                send(two_out.at[k, block(g)], two_in.at[k, block(g)], out_s.at[1], two_r.at[g],
                                     (band, to(k) * pair + b))

    points = 1.0 / float(cols * n_lon)

    def rows_of(d, g):
        return zon.at[pl.ds(d * vp + g * gv, gv)]

    def stage_b(g):
        await_bytes(two_in.at[pl.ds(1, outer - 1), block(g)], two_r.at[g])

        def total(j):
            x = two_out[0, g * gb + j]
            for k in far:
                x = x + two_in[k, g * gb + j]
            return x

        truths = [total(4 * gv + j) for j in range(gb - 4 * gv)]
        for r in range(gv):
            sq, off, pr, sp = [total(4 * r + s) for s in range(4)]
            tr = jnp.broadcast_to(truths[r // leads][r % leads:r % leads + 1, :], (leads, lanes))
            row = me * vp + g * gv + r
            zon[row, 0] = sq * points
            zon[row, 1] = off * points
            zon[row, 2] = pr * points / jnp.sqrt(jnp.maximum(sp * points, FLOOR) * jnp.maximum(tr * points, FLOOR))
        mine = rows_of(me, g)
        for k in far:
            gather_z[g, k] = send(mine, mine, out_s.at[2], agz_r.at[g, k - 1], (band, to(k) * pair + b))
        if pair == 2:
            send(mine, mine, out_s.at[3], agy_r, partner)

    def stage_c(g):
        for k in far:
            gather_z[g, k].wait_recv()
            if pair == 2:
                block_k = rows_of(source(k) * pair + b, g)
                send(block_k, block_k, out_s.at[3], agy_r, partner)

    near = n_lat - 1 + pair - 1

    def gather(first_k, n, r, total):
        if n:
            await_bytes(g_in.at[pl.ds(first_k, n)], r)
        for k in range(first_k, first_k + n):
            total = total + g_in[k]
        return total

    def global_sums():
        for s in range(5):
            d = lax.dot_general(weight, flat[s], (((1,), (1,)), ((), ())), precision=lax.Precision.HIGHEST,
                                preferred_element_type=jnp.float32)
            g_out[0, s:s + 1, 0:leads * wide] = d[0:1, :]
        for k in range(1, n_lat):
            send(g_out.at[0], g_in.at[k - 1], out_s.at[4], g_r.at[0], (lax.rem(band + k, n_lat), me))

    def global_band():
        g_out[1] = gather(0, n_lat - 1, g_r.at[0], g_out[0])
        if pair == 2:
            send(g_out.at[1], g_in.at[n_lat - 1], out_s.at[4], g_r.at[1], partner)

    def global_pair():
        g_out[2] = gather(n_lat - 1, pair - 1, g_r.at[1], g_out[1])
        for k in far:
            send(g_out.at[2], g_in.at[near + k - 1], out_s.at[4], g_r.at[2], (band, to(k) * pair + b))

    def global_scores():
        gs = gather(near, outer - 1, g_r.at[2], g_out[2])
        g_mine[...] = gs / float(total_rows * cols * n_lon)
        mse, off, pr, sp, tr = [g_mine[s:s + 1, :] for s in range(5)]
        rmse = jnp.sqrt(jnp.maximum(mse, FLOOR))
        skill = pr / jnp.sqrt(jnp.maximum(sp, FLOOR) * jnp.maximum(tr, FLOOR))
        for l in range(leads):
            for x, out in ((rmse, g_rmse), (off, g_off), (skill, g_skill)):
                out[l:l + 1, :] = x[:, l * wide:l * wide + nvars]

    for t in range(groups + 2):
        if t < groups:
            stage_a(t)
        if t == 0:
            global_sums()
        if t == groups - 1:
            global_band()
        if 0 <= t - 1 < groups:
            stage_b(t - 1)
        if 0 <= t - 2 < groups:
            stage_c(t - 2)
        if t == groups - 1:
            global_pair()
    global_scores()
    if pair == 2:
        await_bytes(zon.at[pl.ds(0, outer * vp)], agy_r)
        await_bytes(one_in, out_s.at[0])
        await_bytes(zon.at[pl.ds(0, outer * vp)], out_s.at[3])
    await_bytes(two_in.at[pl.ds(1, outer - 1)], out_s.at[1])
    await_bytes(zon.at[pl.ds(0, (outer - 1) * vp)], out_s.at[2])
    await_bytes(g_in, out_s.at[4])


def pieces_of(nvars, n_lon, vp):
    pieces, covered = [], 0
    for d in range(n_lon):
        start = min(d * vp, nvars - vp)
        if start + vp > covered:
            n = start + vp - covered
            src = d * vp + covered - start
            if pieces and pieces[-1][0] + pieces[-1][2] == src:
                pieces[-1][2] += n
            else:
                pieces.append([src, covered, n])
            covered += n
    return pieces


def writer(n_lon, vp, zon, g_rmse, g_off, g_skill, o_sq, o_off, o_skill, o_rmse, o_moff, o_mskill, sem):
    copies = []
    for src, dst, n in pieces_of(o_sq.shape[0], n_lon, vp):
        for m, out in enumerate((o_sq, o_off, o_skill)):
            copies.append((zon.at[pl.ds(src, n), m], out.at[pl.ds(dst, n)]))
    copies += [(g_rmse, o_rmse), (g_off, o_moff), (g_skill, o_mskill)]
    copies = [pltpu.make_async_copy(x, y, sem.at[i]) for i, (x, y) in enumerate(copies)]
    for c in copies:
        c.start()
    for c in copies:
        c.wait()


def local(n_lat, n_lon, pred, ver, norm, flag, par):
    leads, nvars, cols, lanes = pred.shape
    vp = -(-nvars // n_lon)
    pair, outer, groups = split(n_lon, vp)
    blocks = groups * (4 * (vp // groups) - (-(vp // groups) // leads))
    wide = -(-nvars // 8) * 8
    glanes = -(-leads * wide // 128) * 128
    hops = n_lat - 1 + pair - 1 + outer - 1
    f32 = jnp.float32
    dma = pltpu.SemaphoreType.DMA
    vmem = pl.BlockSpec(memory_space=pltpu.VMEM)
    hbm = pl.BlockSpec(memory_space=pl.ANY)
    zonal = jax.ShapeDtypeStruct((nvars, leads, lanes), f32)
    whole = jax.ShapeDtypeStruct((leads, nvars), f32)
    inner = pl.pallas_call(
        functools.partial(kernel, n_lat, n_lon, vp),
        out_shape=(pltpu.VMEM((n_lon * vp, 3, leads, lanes), f32),) + (pltpu.VMEM((leads, nvars), f32),) * 3,
        in_specs=[pl.BlockSpec(memory_space=pltpu.SMEM)] + [hbm] * 4,
        out_specs=(vmem,) * 4,
        scratch_shapes=[
            pltpu.VMEM((n_lon, vp, cols, leads, lanes), f32),
            pltpu.VMEM((cols, nvars, lanes), f32),
            pltpu.VMEM((cols, nvars, lanes), f32),
            pltpu.VMEM((cols, lanes), jnp.int32),
            pltpu.VMEM((cols, lanes), f32),
            pltpu.VMEM((nvars, lanes), f32),
            pltpu.VMEM((n_lon, blocks, leads, lanes), f32),
            pltpu.VMEM((outer, blocks, leads, lanes), f32),
            pltpu.VMEM((outer, blocks, leads, lanes), f32),
            pltpu.VMEM((outer, blocks, leads, lanes), f32),
            pltpu.VMEM((5, leads * wide, lanes), f32),
            pltpu.VMEM((3, 5, glanes), f32),
            pltpu.VMEM((hops, 5, glanes), f32),
            pltpu.VMEM((5, glanes), f32),
            dma((3,)), dma((n_lon,)), dma((5,)),
            dma((groups, outer)), dma((groups,)), dma((groups, outer - 1)), dma, dma((3,)),
        ],
        compiler_params=pltpu.CompilerParams(collective_id=0, has_side_effects=True, vmem_limit_bytes=LIMIT),
    )(par, jnp.transpose(pred, (1, 2, 0, 3)), jnp.transpose(ver, (1, 0, 2)), jnp.transpose(norm, (1, 0, 2)), flag)
    out = pl.pallas_call(
        functools.partial(writer, n_lon, vp),
        out_shape=(zonal,) * 3 + (whole,) * 3,
        in_specs=[vmem] * 4,
        out_specs=(hbm,) * 6,
        scratch_shapes=[dma((3 * len(pieces_of(nvars, n_lon, vp)) + 3,))],
        compiler_params=pltpu.CompilerParams(vmem_limit_bytes=4 << 20),
    )(*inner)
    return tuple(jnp.transpose(x, (1, 0, 2)) for x in out[:3]) + tuple(out[3:])


def solution(mesh):
    n_lat, n_lon = mesh.shape["lat"], mesh.shape["lon"]
    in_specs = (
        P(None, None, "lon", "lat"),
        P(None, "lon", "lat"),
        P(None, "lon", "lat"),
        P("lon", "lat"),
        P(),
    )
    out_specs = (P(None, None, "lat"), P(None, None, "lat"), P(None, None, "lat"), P(), P(), P())
    return jax.shard_map(functools.partial(local, n_lat, n_lon), mesh=mesh, in_specs=in_specs, out_specs=out_specs,
                         check_vma=False)
```

time: 33.6 us -> 30.8 us (0.917)
  Pallas kernels: 32.8 us -> 30 us
    pallas_call x1, Pallas kernels: 31.9 us -> 29.2 us  [local(): pl.pallas_call(functools.partial(kernel, n_lat, n_lon, vp), out_shape=(pl...]
where the time goes in v2:
time: 30.8 us; the launch traced here: 30.7 us
  Pallas kernels  30 us (97%)
  between operations  0.64 us (2%)
    pallas_call x1, Pallas kernels, local(): pl.pallas_call(functools.partial(kernel, n_lat, n_lon, vp), out_shape=(pl...  29.2 us
    pallas_call x1, Pallas kernels, local(): pl.pallas_call(functools.partial(writer, n_lon, vp), out_shape=(zonal,) *...  0.83 us

profile of v2, /device:TPU:0, one launch (start us, length us, event | category | flops | bytes accessed | tf_op | source)
XLA Modules:
  0.0 30.7 jit_solution(9504118155254955949)
XLA Ops:
  0.6 29.2 %shard_map.100 = (f32[72,3,4,128]{3,2,1,0:T(4,128)S(1)}, f32[4,69]{1,0:T(4,128)S(1)}, f32[4,69]{1,0:T(4,128)S(1)}, f32[4,69]{1,0:T(4,128)S(1)}) custom-call(s32[4]{0:T(128)} %par.1, f32[69,45,4,128]{3,2,1,0:T(4,128)} %bitcast.6, f32[45,69,128]{2,1,0:T(8,128)} %bitcast.7, f32[45,69,128]{2,1,0:T(8,128)} %bitcast.8, s32[45,128]{1,0:T(8,128)} %flag.1), custom_call_target="tpu_custom_call" | custom-call | tf_op jit(solution)/shard_map/pallas_call | solution.py:328
  29.8 0.8 %shard_map.101 = (f32[69,4,128]{2,1,0:T(4,128)}, f32[69,4,128]{2,1,0:T(4,128)}, f32[69,4,128]{2,1,0:T(4,128)}, f32[4,69]{1,0:T(4,128)}, f32[4,69]{1,0:T(4,128)}, /*index=5*/f32[4,69]{1,0:T(4,128)}) custom-call(f32[72,3,4,128]{3,2,1,0:T(4,128)S(1)} %get-tuple-element.16.zon, f32[4,69]{1,0:T(4,128)S(1)} %get-tuple-element.17.g_rmse, ...), custom_call_target="tpu_custom_call" | custom-call | tf_op jit(solution)/shard_map/pallas_call | solution.py:353

commit v3 on v2

--- a/solution.py
+++ b/solution.py
@@ -30,7 +30,7 @@
 
 
 def kernel(n_lat, n_lon, vp, par, pred, ver, norm, flag, zon, g_rmse, g_off, g_skill,
-           xp, xv, xn, xf, kf, spread_t, part, one_in, two_out, two_in, flat, g_out, g_in, g_mine,
+           xp, xt, xf, kf, spread_t, part, one_in, two_out, two_in, flat, g_in, g_mine,
            in_sem, pred_sem, out_s, one_r, two_r, agz_r, agy_r, g_r):
     nvars, cols, leads, lanes = pred.shape
     pair, outer, groups = split(n_lon, vp)
@@ -65,19 +65,15 @@
     order = [(k, True) for k in steps] if pair == 2 else []
     base = len(order)
     order += [(k, False) for k in steps]
-    barrier = pltpu.get_barrier_semaphore()
-    for k in range(1, n_lon):
-        pl.semaphore_signal(barrier, inc=1, device_id=(band, lax.rem(me + k, n_lon)), device_id_type=MESH)
-    for k in range(1, n_lat):
-        pl.semaphore_signal(barrier, inc=1, device_id=(lax.rem(band + k, n_lat), me), device_id_type=MESH)
-
-    first = [
-        pltpu.make_async_copy(flag, xf, in_sem.at[0]),
-        pltpu.make_async_copy(norm, xn, in_sem.at[1]),
-        pltpu.make_async_copy(ver, xv, in_sem.at[2]),
-    ]
-    for c in first:
-        c.start()
+    pieces = 3 if cols % 3 == 0 else 1
+    span = cols // pieces
+    xn, xv = xt.at[0], xt.at[1]
+    flags = pltpu.make_async_copy(flag, xf, in_sem.at[pieces])
+    flags.start()
+    for p in range(pieces):
+        here = pl.ds(p * span, span)
+        pltpu.make_async_copy(norm.at[here], xt.at[0, here], in_sem.at[p]).start()
+        pltpu.make_async_copy(ver.at[here], xt.at[1, here], in_sem.at[p]).start()
     chunk_vars, copies = [], []
     for i, (k, away) in enumerate(order):
         v0 = first_var(to(k) * pair + (ob if away else b))
@@ -85,41 +81,48 @@
         copies.append(pltpu.make_async_copy(pred.at[pl.ds(v0, vp)], xp.at[i], pred_sem.at[i]))
     copies[0].start()
 
+    barrier = pltpu.get_barrier_semaphore()
+    for k in range(1, n_lon):
+        pl.semaphore_signal(barrier, inc=1, device_id=(band, lax.rem(me + k, n_lon)), device_id_type=MESH)
+    for k in range(1, n_lat):
+        for there in ([me, a * pair + ob] if pair == 2 else [me]):
+            pl.semaphore_signal(barrier, inc=1, device_id=(lax.rem(band + k, n_lat), there), device_id_type=MESH)
+
     first_row = jnp.int32(0)
     filled = jnp.int32(0)
     for i in range(n_lat):
         first_row = first_row + jnp.where(i < band, par[i], 0)
         filled = filled + jnp.where(i == band, par[i], 0)
-    total_rows = MEAN_ROWS * n_lat + 1
-    slot = lax.broadcasted_iota(jnp.int32, (8, lanes), 1)
-    g_row = (first_row + slot).astype(jnp.float32)
-    normalizer = sum(math.sin(math.pi * r / (total_rows - 1)) for r in range(total_rows))
-    angle = (g_row - 0.5 * (total_rows - 1)) * (math.pi / (total_rows - 1))
-    weight = jnp.where(slot < filled, cosine(angle) * (total_rows / normalizer), 0.0)
     if gv % leads:
         for i in range(n_lon):
             for g in range(groups):
                 part[i, g * gb + gb - 1] = jnp.zeros((leads, lanes), jnp.float32)
 
-    first[0].wait()
+    flags.wait()
     kf[...] = jnp.where(lax.broadcasted_iota(jnp.int32, (cols, lanes), 1) < filled, xf[...].astype(jnp.float32), 0.0)
-    first[1].wait()
-    first[2].wait()
-    for c in copies[1:]:
-        c.start()
 
     def truth_column(c, total):
         t = kf[pl.ds(c, 1), :] * (xv[c] - xn[c])
         xv[c] = t
         return total + t * t
 
-    spread_t[...] = lax.fori_loop(0, cols, truth_column, jnp.zeros((nvars, lanes), jnp.float32))
-
-    def sums(i):
-        copies[i].wait()
+    truth_total = jnp.zeros((nvars, lanes), jnp.float32)
+    for p in range(pieces):
+        here = xt.at[:, pl.ds(p * span, span)]
+        pltpu.make_async_copy(here, here, in_sem.at[p]).wait()
+        if p == 0:
+            for c in copies[1:]:
+                c.start()
+        truth_total = lax.fori_loop(p * span, (p + 1) * span, truth_column, truth_total, unroll=5 if span % 5 == 0 else 1)
+    spread_t[...] = truth_total
+
+    def sums(i, g):
+        if g == 0:
+            copies[i].wait()
         v0 = chunk_vars[i]
 
-        def one(v, carry):
+        def one(r, carry):
+            v = g * gv + r
             sq = off = pr = sp = None
             for c in range(cols):
                 n_ = xn[c, pl.ds(v0 + v, 1), :]
@@ -130,7 +133,7 @@
                     sq, off, pr, sp = e * e, e, f * t_, f * f
                 else:
                     sq, off, pr, sp = sq + e * e, off + e, pr + f * t_, sp + f * f
-            row = v * 4 + (v // gv) * (gb - 4 * gv)
+            row = g * gb + r * 4
             part[i, row] = sq
             part[i, row + 1] = off
             part[i, row + 2] = pr
@@ -140,10 +143,9 @@
                 flat[s, pl.ds(v0 + v, leads, stride=wide), :] = x
             return carry
 
-        lax.fori_loop(0, vp, one, 0)
-        for v in range(vp):
-            g, r = divmod(v, gv)
-            part[i, g * gb + 4 * gv + r // leads, r % leads:r % leads + 1, :] = spread_t[pl.ds(v0 + v, 1), :]
+        lax.fori_loop(0, gv, one, 0)
+        for r in range(gv):
+            part[i, g * gb + 4 * gv + r // leads, r % leads:r % leads + 1, :] = spread_t[pl.ds(v0 + g * gv + r, 1), :]
 
     def block(g):
         return pl.ds(g * gb, gb)
@@ -162,31 +164,29 @@
     def send_one(g, q, k):
         phase_one[g, k] = send(part.at[q, block(g)], one_in.at[k, block(g)], out_s.at[0], one_r.at[g, k], partner)
 
-    greeted = False
-    for q, k in enumerate(steps if pair == 2 else []):
-        sums(q)
+    greeted = []
+
+    def greet():
         if not greeted:
-            pl.semaphore_wait(barrier, n_lon - 1 + n_lat - 1)
-            greeted = True
-        send_one(0, q, k)
-    for g in range(1, groups):
+            pl.semaphore_wait(barrier, n_lon - 1 + (n_lat - 1) * pair)
+            greeted.append(True)
+
+    def away(g):
         for q, k in enumerate(steps if pair == 2 else []):
+            sums(q, g)
+            greet()
             send_one(g, q, k)
 
-    def stage_a(g):
-        for q, k in enumerate(steps):
-            if g == 0:
-                sums(base + q)
-                if base == 0 and q == 0:
-                    pl.semaphore_wait(barrier, n_lon - 1 + n_lat - 1)
-            local = part[base + q, block(g)]
-            if pair == 2:
-                phase_one[g, k].wait_recv()
-                local = local + one_in[k, block(g)]
-            two_out[k, block(g)] = local
-            if k:
-                send(two_out.at[k, block(g)], two_in.at[k, block(g)], out_s.at[1], two_r.at[g],
-                                     (band, to(k) * pair + b))
+    def stage_a(g, q):
+        k = steps[q]
+        greet()
+        local = part[base + q, block(g)]
+        if pair == 2:
+            phase_one[g, k].wait_recv()
+            local = local + one_in[k, block(g)]
+        two_out[k, block(g)] = local
+        if k:
+            send(two_out.at[k, block(g)], two_in.at[k, block(g)], out_s.at[1], two_r.at[g], (band, to(k) * pair + b))
 
     points = 1.0 / float(cols * n_lon)
 
@@ -223,36 +223,40 @@
                 block_k = rows_of(source(k) * pair + b, g)
                 send(block_k, block_k, out_s.at[3], agy_r, partner)
 
-    near = n_lat - 1 + pair - 1
-
-    def gather(first_k, n, r, total):
-        if n:
-            await_bytes(g_in.at[pl.ds(first_k, n)], r)
-        for k in range(first_k, first_k + n):
-            total = total + g_in[k]
-        return total
+    near = n_lat * pair
 
     def global_sums():
+        total_rows = MEAN_ROWS * n_lat + 1
+        slot = lax.broadcasted_iota(jnp.int32, (8, lanes), 1)
+        g_row = (first_row + slot).astype(jnp.float32)
+        normalizer = sum(math.sin(math.pi * r / (total_rows - 1)) for r in range(total_rows))
+        angle = (g_row - 0.5 * (total_rows - 1)) * (math.pi / (total_rows - 1))
+        weight = jnp.where(slot < filled, cosine(angle) * (total_rows / normalizer), 0.0)
         for s in range(5):
             d = lax.dot_general(weight, flat[s], (((1,), (1,)), ((), ())), precision=lax.Precision.HIGHEST,
                                 preferred_element_type=jnp.float32)
-            g_out[0, s:s + 1, 0:leads * wide] = d[0:1, :]
-        for k in range(1, n_lat):
-            send(g_out.at[0], g_in.at[k - 1], out_s.at[4], g_r.at[0], (lax.rem(band + k, n_lat), me))
-
-    def global_band():
-        g_out[1] = gather(0, n_lat - 1, g_r.at[0], g_out[0])
-        if pair == 2:
-            send(g_out.at[1], g_in.at[n_lat - 1], out_s.at[4], g_r.at[1], partner)
-
-    def global_pair():
-        g_out[2] = gather(n_lat - 1, pair - 1, g_r.at[1], g_out[1])
+            g_in[band * pair + b, s:s + 1, 0:leads * wide] = d[0:1, :]
+        mine = g_in.at[band * pair + b]
+        for k in range(1, near):
+            device = (lax.rem(band + k % n_lat, n_lat), me if k < n_lat else a * pair + ob)
+            send(mine, mine, out_s.at[4], g_r.at[0], device)
+
+    def global_near():
+        await_bytes(g_in.at[pl.ds(0, near - 1)], g_r.at[0])
+        total = g_in[0]
+        for k in range(1, near):
+            total = total + g_in[k]
+        mine = g_in.at[near + a]
+        mine[...] = total
         for k in far:
-            send(g_out.at[2], g_in.at[near + k - 1], out_s.at[4], g_r.at[2], (band, to(k) * pair + b))
+            send(mine, mine, out_s.at[4], g_r.at[1], (band, to(k) * pair + b))
 
     def global_scores():
-        gs = gather(near, outer - 1, g_r.at[2], g_out[2])
-        g_mine[...] = gs / float(total_rows * cols * n_lon)
+        await_bytes(g_in.at[pl.ds(near, outer - 1)], g_r.at[1])
+        total = g_in[near]
+        for k in range(1, outer):
+            total = total + g_in[near + k]
+        g_mine[...] = total / float((MEAN_ROWS * n_lat + 1) * cols * n_lon)
         mse, off, pr, sp, tr = [g_mine[s:s + 1, :] for s in range(5)]
         rmse = jnp.sqrt(jnp.maximum(mse, FLOOR))
         skill = pr / jnp.sqrt(jnp.maximum(sp, FLOOR) * jnp.maximum(tr, FLOOR))
@@ -260,19 +264,22 @@
             for x, out in ((rmse, g_rmse), (off, g_off), (skill, g_skill)):
                 out[l:l + 1, :] = x[:, l * wide:l * wide + nvars]
 
-    for t in range(groups + 2):
-        if t < groups:
-            stage_a(t)
-        if t == 0:
-            global_sums()
-        if t == groups - 1:
-            global_band()
-        if 0 <= t - 1 < groups:
-            stage_b(t - 1)
-        if 0 <= t - 2 < groups:
-            stage_c(t - 2)
-        if t == groups - 1:
-            global_pair()
+    away(0)
+    for q in range(outer):
+        sums(base + q, 0)
+    for g in range(1, groups):
+        away(g)
+        for q in range(outer):
+            stage_a(g - 1, q)
+            sums(base + q, g)
+    global_sums()
+    for q in range(outer):
+        stage_a(groups - 1, q)
+    for g in range(groups):
+        stage_b(g)
+    global_near()
+    for g in range(groups):
+        stage_c(g)
     global_scores()
     if pair == 2:
         await_bytes(zon.at[pl.ds(0, outer * vp)], agy_r)
@@ -280,7 +287,7 @@
         await_bytes(zon.at[pl.ds(0, outer * vp)], out_s.at[3])
     await_bytes(two_in.at[pl.ds(1, outer - 1)], out_s.at[1])
     await_bytes(zon.at[pl.ds(0, (outer - 1) * vp)], out_s.at[2])
-    await_bytes(g_in, out_s.at[4])
+    await_bytes(g_in.at[pl.ds(0, near + outer - 2)], out_s.at[4])
 
 
 def pieces_of(nvars, n_lon, vp):
@@ -318,7 +325,7 @@
     blocks = groups * (4 * (vp // groups) - (-(vp // groups) // leads))
     wide = -(-nvars // 8) * 8
     glanes = -(-leads * wide // 128) * 128
-    hops = n_lat - 1 + pair - 1 + outer - 1
+    hops = n_lat * pair + outer
     f32 = jnp.float32
     dma = pltpu.SemaphoreType.DMA
     vmem = pl.BlockSpec(memory_space=pltpu.VMEM)
@@ -332,8 +339,7 @@
         out_specs=(vmem,) * 4,
         scratch_shapes=[
             pltpu.VMEM((n_lon, vp, cols, leads, lanes), f32),
-            pltpu.VMEM((cols, nvars, lanes), f32),
-            pltpu.VMEM((cols, nvars, lanes), f32),
+            pltpu.VMEM((2, cols, nvars, lanes), f32),
             pltpu.VMEM((cols, lanes), jnp.int32),
             pltpu.VMEM((cols, lanes), f32),
             pltpu.VMEM((nvars, lanes), f32),
@@ -342,11 +348,10 @@
             pltpu.VMEM((outer, blocks, leads, lanes), f32),
             pltpu.VMEM((outer, blocks, leads, lanes), f32),
             pltpu.VMEM((5, leads * wide, lanes), f32),
-            pltpu.VMEM((3, 5, glanes), f32),
             pltpu.VMEM((hops, 5, glanes), f32),
             pltpu.VMEM((5, glanes), f32),
-            dma((3,)), dma((n_lon,)), dma((5,)),
-            dma((groups, outer)), dma((groups,)), dma((groups, outer - 1)), dma, dma((3,)),
+            dma((4,)), dma((n_lon,)), dma((5,)),
+            dma((groups, outer)), dma((groups,)), dma((groups, outer - 1)), dma, dma((2,)),
         ],
         compiler_params=pltpu.CompilerParams(collective_id=0, has_side_effects=True, vmem_limit_bytes=LIMIT),
     )(par, jnp.transpose(pred, (1, 2, 0, 3)), jnp.transpose(ver, (1, 0, 2)), jnp.transpose(norm, (1, 0, 2)), flag)

time: 30.8 us -> 28.8 us (0.935)
  Pallas kernels: 30 us -> 28 us
    pallas_call x1, Pallas kernels: 29.2 us -> 27.2 us  [local(): pl.pallas_call(functools.partial(kernel, n_lat, n_lon, vp), out_shape=(pl...]
where the time goes in v3:
time: 28.8 us; the launch traced here: 28.6 us
  Pallas kernels  28 us (97%)
  between operations  0.64 us (2%)
    pallas_call x1, Pallas kernels, local(): pl.pallas_call(functools.partial(kernel, n_lat, n_lon, vp), out_shape=(pl...  27.2 us
    pallas_call x1, Pallas kernels, local(): pl.pallas_call(functools.partial(writer, n_lon, vp), out_shape=(zonal,) *...  0.83 us

profile of v3, /device:TPU:0, one launch (start us, length us, event | category | flops | bytes accessed | tf_op | source)
XLA Modules:
  0.0 28.6 jit_solution(5581665805645661734)
XLA Ops:
  0.6 27.2 %shard_map.100 = (f32[72,3,4,128]{3,2,1,0:T(4,128)S(1)}, f32[4,69]{1,0:T(4,128)S(1)}, f32[4,69]{1,0:T(4,128)S(1)}, f32[4,69]{1,0:T(4,128)S(1)}) custom-call(s32[4]{0:T(128)} %par.1, f32[69,45,4,128]{3,2,1,0:T(4,128)} %bitcast.6, f32[45,69,128]{2,1,0:T(8,128)} %bitcast.7, f32[45,69,128]{2,1,0:T(8,128)} %bitcast.8, s32[45,128]{1,0:T(8,128)} %flag.1), custom_call_target="tpu_custom_call" | custom-call | tf_op jit(solution)/shard_map/pallas_call | solution.py:335
  27.8 0.8 %shard_map.101 = (f32[69,4,128]{2,1,0:T(4,128)}, f32[69,4,128]{2,1,0:T(4,128)}, f32[69,4,128]{2,1,0:T(4,128)}, f32[4,69]{1,0:T(4,128)}, f32[4,69]{1,0:T(4,128)}, /*index=5*/f32[4,69]{1,0:T(4,128)}) custom-call(f32[72,3,4,128]{3,2,1,0:T(4,128)S(1)} %get-tuple-element.16.zon, f32[4,69]{1,0:T(4,128)S(1)} %get-tuple-element.17.g_rmse, ...), custom_call_target="tpu_custom_call" | custom-call | tf_op jit(solution)/shard_map/pallas_call | solution.py:358

commit v4 on v3

--- a/solution.py
+++ b/solution.py
@@ -23,19 +23,31 @@
     return total
 
 
-def split(n_lon, vp):
+def split(n_lon):
     pair = 2 if n_lon % 2 == 0 else 1
-    groups = max(g for g in (1, 2, 3) if vp % g == 0)
-    return pair, n_lon // pair, groups
+    return pair, n_lon // pair
+
+
+def plan(vp):
+    if vp > 4:
+        return [vp // 3, vp - vp // 3 - 2, 2]
+    return [1] * vp
+
+
+def rows_in(sizes, leads):
+    return [4 * w - (-w // leads) for w in sizes]
 
 
 def kernel(n_lat, n_lon, vp, par, pred, ver, norm, flag, zon, g_rmse, g_off, g_skill,
            xp, xt, xf, kf, spread_t, part, one_in, two_out, two_in, flat, g_in, g_mine,
            in_sem, pred_sem, out_s, one_r, two_r, agz_r, agy_r, g_r):
     nvars, cols, leads, lanes = pred.shape
-    pair, outer, groups = split(n_lon, vp)
-    gv = vp // groups
-    gb = 4 * gv - (-gv // leads)
+    pair, outer = split(n_lon)
+    sizes = plan(vp)
+    groups = len(sizes)
+    off = [sum(sizes[:g]) for g in range(groups)]
+    gbs = rows_in(sizes, leads)
+    row_of = [sum(gbs[:g]) for g in range(groups)]
     band = lax.axis_index("lat")
     me = lax.axis_index("lon")
     a, b = me // pair, me % pair
@@ -93,10 +105,10 @@
     for i in range(n_lat):
         first_row = first_row + jnp.where(i < band, par[i], 0)
         filled = filled + jnp.where(i == band, par[i], 0)
-    if gv % leads:
-        for i in range(n_lon):
-            for g in range(groups):
-                part[i, g * gb + gb - 1] = jnp.zeros((leads, lanes), jnp.float32)
+    for g in range(groups):
+        if sizes[g] % leads:
+            for i in range(n_lon):
+                part[i, row_of[g] + gbs[g] - 1] = jnp.zeros((leads, lanes), jnp.float32)
 
     flags.wait()
     kf[...] = jnp.where(lax.broadcasted_iota(jnp.int32, (cols, lanes), 1) < filled, xf[...].astype(jnp.float32), 0.0)
@@ -116,39 +128,42 @@
         truth_total = lax.fori_loop(p * span, (p + 1) * span, truth_column, truth_total, unroll=5 if span % 5 == 0 else 1)
     spread_t[...] = truth_total
 
+    landed = []
+
     def sums(i, g):
-        if g == 0:
+        if i not in landed:
             copies[i].wait()
+            landed.append(i)
         v0 = chunk_vars[i]
 
         def one(r, carry):
-            v = g * gv + r
-            sq = off = pr = sp = None
+            v = off[g] + r
+            sq = off_ = pr = sp = None
             for c in range(cols):
                 n_ = xn[c, pl.ds(v0 + v, 1), :]
                 t_ = xv[c, pl.ds(v0 + v, 1), :]
                 f = kf[c:c + 1, :] * (xp[i, v, c] - n_)
                 e = f - t_
                 if sq is None:
-                    sq, off, pr, sp = e * e, e, f * t_, f * f
+                    sq, off_, pr, sp = e * e, e, f * t_, f * f
                 else:
-                    sq, off, pr, sp = sq + e * e, off + e, pr + f * t_, sp + f * f
-            row = g * gb + r * 4
+                    sq, off_, pr, sp = sq + e * e, off_ + e, pr + f * t_, sp + f * f
+            row = row_of[g] + r * 4
             part[i, row] = sq
-            part[i, row + 1] = off
+            part[i, row + 1] = off_
             part[i, row + 2] = pr
             part[i, row + 3] = sp
             tr = jnp.broadcast_to(spread_t[pl.ds(v0 + v, 1), :], (leads, lanes))
-            for s, x in enumerate((sq, off, pr, sp, tr)):
+            for s, x in enumerate((sq, off_, pr, sp, tr)):
                 flat[s, pl.ds(v0 + v, leads, stride=wide), :] = x
             return carry
 
-        lax.fori_loop(0, gv, one, 0)
-        for r in range(gv):
-            part[i, g * gb + 4 * gv + r // leads, r % leads:r % leads + 1, :] = spread_t[pl.ds(v0 + g * gv + r, 1), :]
+        lax.fori_loop(0, sizes[g], one, 0)
+        for r in range(sizes[g]):
+            part[i, row_of[g] + 4 * sizes[g] + r // leads, r % leads:r % leads + 1, :] = spread_t[pl.ds(v0 + off[g] + r, 1), :]
 
     def block(g):
-        return pl.ds(g * gb, gb)
+        return pl.ds(row_of[g], gbs[g])
 
     def send(src, dst, s, r, device):
         c = pltpu.make_async_remote_copy(src_ref=src, dst_ref=dst, send_sem=s, recv_sem=r, device_id=device, device_id_type=MESH)
@@ -171,11 +186,11 @@
             pl.semaphore_wait(barrier, n_lon - 1 + (n_lat - 1) * pair)
             greeted.append(True)
 
-    def away(g):
-        for q, k in enumerate(steps if pair == 2 else []):
+    def away(g, q):
+        if pair == 2:
             sums(q, g)
             greet()
-            send_one(g, q, k)
+            send_one(g, q, steps[q])
 
     def stage_a(g, q):
         k = steps[q]
@@ -191,35 +206,42 @@
     points = 1.0 / float(cols * n_lon)
 
     def rows_of(d, g):
-        return zon.at[pl.ds(d * vp + g * gv, gv)]
+        return zon.at[pl.ds(d * vp + off[g], sizes[g])]
+
+    def straight(g):
+        return pair == 2 and g == groups - 1
 
     def stage_b(g):
+        gv = sizes[g]
         await_bytes(two_in.at[pl.ds(1, outer - 1), block(g)], two_r.at[g])
 
         def total(j):
-            x = two_out[0, g * gb + j]
+            x = two_out[0, row_of[g] + j]
             for k in far:
-                x = x + two_in[k, g * gb + j]
+                x = x + two_in[k, row_of[g] + j]
             return x
 
-        truths = [total(4 * gv + j) for j in range(gb - 4 * gv)]
+        truths = [total(4 * gv + j) for j in range(gbs[g] - 4 * gv)]
         for r in range(gv):
-            sq, off, pr, sp = [total(4 * r + s) for s in range(4)]
+            sq, off_, pr, sp = [total(4 * r + s) for s in range(4)]
             tr = jnp.broadcast_to(truths[r // leads][r % leads:r % leads + 1, :], (leads, lanes))
-            row = me * vp + g * gv + r
+            row = me * vp + off[g] + r
             zon[row, 0] = sq * points
-            zon[row, 1] = off * points
+            zon[row, 1] = off_ * points
             zon[row, 2] = pr * points / jnp.sqrt(jnp.maximum(sp * points, FLOOR) * jnp.maximum(tr * points, FLOOR))
         mine = rows_of(me, g)
         for k in far:
             gather_z[g, k] = send(mine, mine, out_s.at[2], agz_r.at[g, k - 1], (band, to(k) * pair + b))
         if pair == 2:
             send(mine, mine, out_s.at[3], agy_r, partner)
+            if straight(g):
+                for k in far:
+                    send(mine, mine, out_s.at[3], agy_r, (band, to(k) * pair + ob))
 
     def stage_c(g):
         for k in far:
             gather_z[g, k].wait_recv()
-            if pair == 2:
+            if pair == 2 and not straight(g):
                 block_k = rows_of(source(k) * pair + b, g)
                 send(block_k, block_k, out_s.at[3], agy_r, partner)
 
@@ -257,27 +279,29 @@
         for k in range(1, outer):
             total = total + g_in[near + k]
         g_mine[...] = total / float((MEAN_ROWS * n_lat + 1) * cols * n_lon)
-        mse, off, pr, sp, tr = [g_mine[s:s + 1, :] for s in range(5)]
+        mse, off_, pr, sp, tr = [g_mine[s:s + 1, :] for s in range(5)]
         rmse = jnp.sqrt(jnp.maximum(mse, FLOOR))
         skill = pr / jnp.sqrt(jnp.maximum(sp, FLOOR) * jnp.maximum(tr, FLOOR))
         for l in range(leads):
-            for x, out in ((rmse, g_rmse), (off, g_off), (skill, g_skill)):
+            for x, out in ((rmse, g_rmse), (off_, g_off), (skill, g_skill)):
                 out[l:l + 1, :] = x[:, l * wide:l * wide + nvars]
 
-    away(0)
+    for q in range(outer):
+        away(0, q)
     for q in range(outer):
         sums(base + q, 0)
     for g in range(1, groups):
-        away(g)
         for q in range(outer):
+            away(g, q)
             stage_a(g - 1, q)
             sums(base + q, g)
     global_sums()
     for q in range(outer):
         stage_a(groups - 1, q)
     for g in range(groups):
+        if g == groups - 1:
+            global_near()
         stage_b(g)
-    global_near()
     for g in range(groups):
         stage_c(g)
     global_scores()
@@ -321,8 +345,10 @@
 def local(n_lat, n_lon, pred, ver, norm, flag, par):
     leads, nvars, cols, lanes = pred.shape
     vp = -(-nvars // n_lon)
-    pair, outer, groups = split(n_lon, vp)
-    blocks = groups * (4 * (vp // groups) - (-(vp // groups) // leads))
+    pair, outer = split(n_lon)
+    sizes = plan(vp)
+    groups = len(sizes)
+    blocks = sum(rows_in(sizes, leads))
     wide = -(-nvars // 8) * 8
     glanes = -(-leads * wide // 128) * 128
     hops = n_lat * pair + outer

time: 28.8 us -> 27.8 us (0.965)
  Pallas kernels: 28 us -> 27 us
    pallas_call x1, Pallas kernels: 27.2 us -> 26.2 us  [local(): pl.pallas_call(functools.partial(kernel, n_lat, n_lon, vp), out_shape=(pl...]
where the time goes in v4:
time: 27.8 us; the launch traced here: 27.6 us
  Pallas kernels  27 us (97%)
  between operations  0.64 us (2%)
    pallas_call x1, Pallas kernels, local(): pl.pallas_call(functools.partial(kernel, n_lat, n_lon, vp), out_shape=(pl...  26.2 us
    pallas_call x1, Pallas kernels, local(): pl.pallas_call(functools.partial(writer, n_lon, vp), out_shape=(zonal,) *...  0.83 us

profile of v4, /device:TPU:0, one launch (start us, length us, event | category | flops | bytes accessed | tf_op | source)
XLA Modules:
  0.0 27.6 jit_solution(308180894226391322)
XLA Ops:
  0.6 26.2 %shard_map.100 = (f32[72,3,4,128]{3,2,1,0:T(4,128)S(1)}, f32[4,69]{1,0:T(4,128)S(1)}, f32[4,69]{1,0:T(4,128)S(1)}, f32[4,69]{1,0:T(4,128)S(1)}) custom-call(s32[4]{0:T(128)} %par.1, f32[69,45,4,128]{3,2,1,0:T(4,128)} %bitcast.6, f32[45,69,128]{2,1,0:T(8,128)} %bitcast.7, f32[45,69,128]{2,1,0:T(8,128)} %bitcast.8, s32[45,128]{1,0:T(8,128)} %flag.1), custom_call_target="tpu_custom_call" | custom-call | tf_op jit(solution)/shard_map/pallas_call | solution.py:361
  26.8 0.8 %shard_map.101 = (f32[69,4,128]{2,1,0:T(4,128)}, f32[69,4,128]{2,1,0:T(4,128)}, f32[69,4,128]{2,1,0:T(4,128)}, f32[4,69]{1,0:T(4,128)}, f32[4,69]{1,0:T(4,128)}, /*index=5*/f32[4,69]{1,0:T(4,128)}) custom-call(f32[72,3,4,128]{3,2,1,0:T(4,128)S(1)} %get-tuple-element.16.zon, f32[4,69]{1,0:T(4,128)S(1)} %get-tuple-element.17.g_rmse, ...), custom_call_target="tpu_custom_call" | custom-call | tf_op jit(solution)/shard_map/pallas_call | solution.py:384
